TPU v7x, 32 devices: a whole 2x2x4 slice. The times are simulated.
32 devices in a mesh: fluid: 16 (over z, x, core), solid: 2 (over y).
Axes of the slice: x: 2, y: 2, z: 4, core: 2. Of those that a mesh axis runs over, the one named last changes fastest.
Arguments:
- fluid_load: float32 [2048, 3, 128], P(('fluid', 'solid')), may hold values from -6 to 6
- stiffness: float32 [2048, 3, 128], P(('fluid', 'solid')), may hold values from 0.2 to 2
- mapping: bfloat16 [2048, 128, 128], P(('fluid', 'solid')), may hold values from -0.5 to 0.5
- live_count: int32 [32], P(('fluid', 'solid')), may hold values from 40 to 64, as said below
- dest_device: int32 [2048, 1], P(('fluid', 'solid')), may hold values from 0 to 15; in each aligned block of 64 rows (0 to 63, 64 to 127, ...) at most 8 rows name the same one
- local_block: int32 [2048], P(('fluid', 'solid')), may hold values from 0 to 3
- compliance: float32 [2, 64, 3, 128], P('solid', 'fluid'), may hold values from 0.05 to 0.5
- start_disp: float32 [2, 64, 3, 128], P('solid', 'fluid'), may hold values from -40 to 40
- residual_history: float32 [50, 2, 64, 3, 128], P(None, 'solid', 'fluid'), may hold values from -40 to 40
- update_history: float32 [50, 2, 64, 3, 128], P(None, 'solid', 'fluid'), may hold values from -2.4 to 2.4
Outputs:
- displacement: float32 [2, 64, 3, 128], P('solid', 'fluid')
- fluid_displacement: float32 [2048, 3, 128], P(('fluid', 'solid'))
Inputs may be any that keep to these rules, and one draw needn't show every extreme that they name: `live_count`: each device's live blocks are its first ones; some device has exactly 64. `dest_device`: among the 64 rows of one device no fluid index appears more than 8 times.
All inputs are finite; a program needn't handle non-finite values.
Results may differ from a plain program's by a relative error of at most 0.0094.
Values may be sent and summed in bfloat16 or wider, within the bound.
A program may use at most 64 MiB of HBM per device.

v0:
```python
import jax
import jax.numpy as jnp
from jax import lax
from jax.sharding import PartitionSpec as P

ITERS = 2


ridge_share = 0.01


def solve_small(gram_matrix, right_side):
    order = gram_matrix.shape[0]
    ridge = ridge_share * jnp.trace(gram_matrix) / order
    factor = jnp.linalg.cholesky(gram_matrix + ridge * jnp.eye(order, dtype=gram_matrix.dtype))
    halfway = lax.linalg.triangular_solve(factor, right_side[:, None], left_side=True, lower=True)
    solved = lax.linalg.triangular_solve(
        factor, halfway, left_side=True, lower=True, transpose_a=True
    )
    return -solved[:, 0]


def full_sums(basis_flat, resid_flat):
    gram_local = jnp.dot(basis_flat, basis_flat.T, precision=lax.Precision.HIGHEST)
    right_local = jnp.dot(basis_flat, resid_flat, precision=lax.Precision.HIGHEST)
    return lax.psum((gram_local, right_local), ("fluid", "solid"))


def body(
    fluid_load,
    stiffness,
    mapping,
    live_count,
    dest_device,
    local_block,
    compliance,
    start_disp,
    residual_history,
    update_history,
):
    blocks = mapping.shape[0]
    struct_width = mapping.shape[1]
    sub_blocks = compliance.shape[1]
    fluid_size = lax.axis_size("fluid")
    alive = (jnp.arange(blocks) < live_count[0]).astype(jnp.float32)[:, None, None]
    capacity = max(2, 2 * ((blocks + fluid_size - 1) // fluid_size))
    dest_hot = (dest_device[:, 0][:, None] == jnp.arange(fluid_size)[None, :]).astype(jnp.int32)
    slot_rank = jnp.sum((jnp.cumsum(dest_hot, axis=0) - 1) * dest_hot, axis=1)
    slot_index = dest_device[:, 0] * capacity + slot_rank
    slot_hot = jnp.arange(fluid_size * capacity)[:, None] == slot_index[None, :]
    sent_ids = jnp.sum(slot_hot.astype(jnp.int32) * (local_block + 1)[None, :], axis=1) - 1
    owner_ids = lax.all_to_all(
        sent_ids.reshape(fluid_size, capacity), "fluid", split_axis=0, concat_axis=0, tiled=True
    )
    owner_hot = owner_ids.reshape(-1)[None, :] == jnp.arange(sub_blocks)[:, None]

    def to_fluid(struct_disp):
        packed = struct_disp[0].astype(jnp.bfloat16)
        chosen = jnp.einsum(
            "ks,kcj->scj",
            owner_hot.astype(jnp.bfloat16),
            packed,
            preferred_element_type=jnp.float32,
        ).astype(jnp.bfloat16)
        returned = lax.all_to_all(
            chosen.reshape(fluid_size, capacity, 3, struct_width),
            "fluid",
            split_axis=0,
            concat_axis=0,
            tiled=True,
        )
        picked = jnp.einsum(
            "sb,scj->bcj",
            slot_hot.astype(jnp.bfloat16),
            returned.reshape(-1, 3, struct_width),
            preferred_element_type=jnp.float32,
        )
        fluid_disp = jnp.einsum(
            "bjn,bcj->bcn", mapping, picked.astype(jnp.bfloat16), preferred_element_type=jnp.float32
        )
        return fluid_disp * alive

    struct_disp = start_disp
    basis_cols = residual_history
    updates = update_history
    last_resid = struct_disp
    last_image = struct_disp
    gram_matrix = None
    for iteration in range(ITERS):
        fluid_disp = to_fluid(struct_disp)
        fluid_force = (alive * (fluid_load - stiffness * fluid_disp)).astype(jnp.bfloat16)
        contrib = jnp.einsum(
            "bjn,bcn->bcj", mapping, fluid_force, preferred_element_type=jnp.float32
        )
        buffer = jnp.einsum(
            "sb,bcj->scj", slot_hot.astype(jnp.float32), contrib, precision=lax.Precision.HIGHEST
        )
        received = lax.all_to_all(
            buffer.reshape(fluid_size, capacity, 3, struct_width),
            "fluid",
            split_axis=0,
            concat_axis=0,
            tiled=True,
        )
        summed = jnp.einsum(
            "ks,scj->kcj",
            owner_hot.astype(jnp.float32),
            received.reshape(-1, 3, struct_width),
            precision=lax.Precision.HIGHEST,
        )
        struct_image = compliance * summed[None]
        residual = struct_image - struct_disp
        newest = residual - last_resid
        if iteration > 0:
            basis_cols = jnp.concatenate([basis_cols[1:], newest[None]], 0)
            updates = jnp.concatenate([updates[1:], (struct_image - last_image)[None]], 0)
        basis_flat = basis_cols.reshape(basis_cols.shape[0], -1)
        resid_flat = residual.reshape(-1)
        gram_matrix, right_side = full_sums(basis_flat, resid_flat)
        coefficients = solve_small(gram_matrix, right_side)
        struct_disp = struct_image + jnp.tensordot(
            coefficients, updates, axes=1, precision=lax.Precision.HIGHEST
        )
        last_resid = residual
        last_image = struct_image
    final_disp = to_fluid(struct_disp)
    return (struct_disp, final_disp)


def solution(mesh):
    in_specs = (
        P(("fluid", "solid"), None, None),
        P(("fluid", "solid"), None, None),
        P(("fluid", "solid"), None, None),
        P(("fluid", "solid")),
        P(("fluid", "solid"), None),
        P(("fluid", "solid")),
        P("solid", "fluid", None, None),
        P("solid", "fluid", None, None),
        P(None, "solid", "fluid", None, None),
        P(None, "solid", "fluid", None, None),
    )
    out_specs = (P("solid", "fluid", None, None), P(("fluid", "solid"), None, None))
    return jax.shard_map(body, mesh=mesh, in_specs=in_specs, out_specs=out_specs, check_vma=False)
```

profile of v0, /device:TPU:0, one launch (start us, length us, event | category | flops | bytes accessed | tf_op | source)
XLA Modules:
  0.0 190.6 jit_solution(16942165006575213732)
XLA Ops:
  0.6 0.0 copy-start
  0.6 0.9 fusion.48
  1.5 0.1 reduce_window_sum.11
  1.6 0.8 select_reduce_fusion.1
  2.5 0.7 multiply_add_fusion
  3.1 0.1 select_reduce_fusion
  3.2 0.1 sub.30
  3.3 13.6 %all_to_all.31 = s32[16,1,8]{2,1,0:T(1,128)S(1)} all-to-all(s32[16,1,8]{2,1,0:T(1,128)S(1)} %bitcast.179), channel_id=1, replica_groups=mesh['fluid'=16,'solid'=2] {'fluid'}, dimensions={0} | all-to-all | bytes 1024 | tf_op jit(solution)/shard_map/all_to_all | solution.py:52
  17.0 0.5 broadcast.90
  17.5 0.7 reduce.7
  18.1 0.1 eq.60
  18.2 0.9 fusion.8
  19.2 0.7 copy.39
  19.8 3.5 %all-to-all-start.1 = ((bf16[16,8,3,128]{3,1,2,0:T(8,128)(2,1)}), bf16[16,8,3,128]{3,1,2,0:T(8,128)(2,1)S(1)}, u32[]{:S(2)}, u32[]{:S(2)}) async-start(bf16[16,8,3,128]{3,1,2,0:T(8,128)(2,1)} %copy.39), calls=%async_computation.1 | async-start | bytes 196608 | tf_op jit(solution)/shard_map/all_to_all | solution.py:65
  24.0 6.7 %all-to-all-done.1 = bf16[16,8,3,128]{3,1,2,0:T(8,128)(2,1)S(1)} async-done(((bf16[16,8,3,128]{3,1,2,0:T(8,128)(2,1)}), bf16[16,8,3,128]{3,1,2,0:T(8,128)(2,1)S(1)}, u32[]{:S(2)}, u32[]{:S(2)}) %all-to-all-start.1) | async-done | bytes 98336 | tf_op jit(solution)/shard_map/all_to_all | solution.py:65
  30.7 0.2 convolution_convert_fusion.5
  30.9 0.0 copy-start.1
  30.9 0.0 copy-start.6
  30.9 2.7 %fusion.12 = f32[64,3,128]{2,1,0:T(4,128)S(1)} fusion(bf16[64,128,128]{2,1,0:T(8,128)(2,1)S(1)} %copy-done, f32[64,3,128]{2,0,1:T(8,128)} %param.15, f32[64,3,128]{2,0,1:T(8,128)} %param.16, bf16[64,3,128]{2,0,1:T(8,128)(2,1)S(1)} %convolution_convert_fusion.5, f32[64]{0:T(128)S(1)} %compare_convert_fusion), kind=kOutput, calls=%fused_computation.23 | convolution fusion | flops 12705792 | bytes 2441472 | tf_op jit(solution)/shard_map/bjn,bcn->bcj/dot_general | solution.py:92
  33.7 0.4 convolution_bitcast_fusion.1
  34.0 0.7 copy.45
  34.7 3.5 %all-to-all-start.2 = ((f32[16,8,3,128]{3,1,2,0:T(8,128)}), f32[16,8,3,128]{3,1,2,0:T(8,128)S(1)}, u32[]{:S(2)}, u32[]{:S(2)}) async-start(f32[16,8,3,128]{3,1,2,0:T(8,128)} %copy.45), calls=%async_computation.2 | async-start | bytes 393216 | tf_op jit(solution)/shard_map/all_to_all | solution.py:98
  38.3 0.4 convolution_bitcast_fusion.3
  38.7 8.5 %all-to-all-done.2 = f32[16,8,3,128]{3,1,2,0:T(8,128)S(1)} async-done(((f32[16,8,3,128]{3,1,2,0:T(8,128)}), f32[16,8,3,128]{3,1,2,0:T(8,128)S(1)}, u32[]{:S(2)}, u32[]{:S(2)}) %all-to-all-start.2) | async-done | bytes 196640 | tf_op jit(solution)/shard_map/all_to_all | solution.py:98
  47.2 0.2 fusion.84
  47.4 0.4 convolution_bitcast_fusion.7
  47.7 37.9 %all-reduce.1 = (f32[50,1]{0,1:T(1,128)S(1)}, f32[50,50]{0,1:T(8,128)S(1)}) all-reduce(f32[50,1]{0,1:T(1,128)S(1)} %convolution_bitcast_fusion.7, f32[50,50]{0,1:T(8,128)S(1)} %convolution_bitcast_fusion.3), channel_id=1, replica_groups=mesh['fluid'=16,'solid'=2] {'fluid','solid'}, use_global_device_ids=true, to_apply=%region_7.9 | all-reduce | flops 2550 | bytes 20400 | tf_op jit(solution)/shard_map/psum | solution.py:26
  85.6 0.6 select_reduce_fusion.5
  86.9 0.1 copy.50
  87.0 4.6 %cholesky.44 = f32[50,50]{1,0:T(8,128)S(1)} custom-call(f32[50,50]{1,0:T(8,128)S(1)} %fusion.62), custom_call_target="Cholesky" | custom-call | tf_op jit(solution)/shard_map/jit(cholesky)/cholesky | solution.py:15
  91.6 0.6 compare_reduce_fusion.1
  92.3 0.7 fusion.55
  92.9 3.8 %custom-call.11 = f32[1,50,50]{1,2,0:T(8,128)S(1)} custom-call(f32[1,50,50]{2,1,0:T(8,128)S(1)} %fusion.55), custom_call_target="InvertDiagBlocksLowerTriangular" | custom-call | tf_op jit(solution)/shard_map/triangular_solve/custom-call.2 | solution.py:17
  96.8 0.2 convolution_bitcast_fusion.11
  96.9 0.2 fusion.18
  97.1 0.3 fusion.21
  97.4 0.3 fusion.9
  97.7 12.5 %all_to_all.32 = bf16[16,8,3,128]{3,1,2,0:T(8,128)(2,1)S(1)} all-to-all(bf16[16,8,3,128]{3,1,2,0:T(8,128)(2,1)S(1)} %copy.51), channel_id=1, replica_groups=mesh['fluid'=16,'solid'=2] {'fluid'}, dimensions={0} | all-to-all | bytes 196608 | tf_op jit(solution)/shard_map/all_to_all | solution.py:65
  110.1 0.2 convolution_convert_fusion.4
  110.4 1.7 fusion.11
  112.1 0.4 convolution_bitcast_fusion
  112.5 0.7 copy.57
  113.2 3.5 %all-to-all-start.4 = ((f32[16,8,3,128]{3,1,2,0:T(8,128)}), f32[16,8,3,128]{3,1,2,0:T(8,128)S(1)}, u32[]{:S(2)}, u32[]{:S(2)}) async-start(f32[16,8,3,128]{3,1,2,0:T(8,128)} %copy.57), calls=%async_computation.4 | async-start | bytes 393216 | tf_op jit(solution)/shard_map/all_to_all | solution.py:98
  116.8 8.8 %all-to-all-done.4 = f32[16,8,3,128]{3,1,2,0:T(8,128)S(1)} async-done(((f32[16,8,3,128]{3,1,2,0:T(8,128)}), f32[16,8,3,128]{3,1,2,0:T(8,128)S(1)}, u32[]{:S(2)}, u32[]{:S(2)}) %all-to-all-start.4) | async-done | bytes 196640 | tf_op jit(solution)/shard_map/all_to_all | solution.py:98
  125.6 0.2 fusion.13
  125.8 0.4 convolution_bitcast_fusion.2
  126.3 0.4 convolution_bitcast_fusion.6
  126.6 37.9 %all-reduce = (f32[50,1]{0,1:T(1,128)S(1)}, f32[50,50]{0,1:T(8,128)S(1)}) all-reduce(f32[50,1]{0,1:T(1,128)S(1)} %convolution_bitcast_fusion.6, f32[50,50]{0,1:T(8,128)S(1)} %convolution_bitcast_fusion.2), channel_id=1, replica_groups=mesh['fluid'=16,'solid'=2] {'fluid','solid'}, use_global_device_ids=true, to_apply=%region_10.14 | all-reduce | flops 2550 | bytes 20400 | tf_op jit(solution)/shard_map/psum | solution.py:26
  164.5 0.6 select_reduce_fusion.4
  165.8 0.1 copy.62
  165.9 4.6 %cholesky.55 = f32[50,50]{1,0:T(8,128)S(1)} custom-call(f32[50,50]{1,0:T(8,128)S(1)} %fusion.59), custom_call_target="Cholesky" | custom-call | tf_op jit(solution)/shard_map/jit(cholesky)/cholesky | solution.py:15
  170.5 0.6 compare_reduce_fusion
  171.2 0.7 fusion.56
  171.8 3.8 %custom-call.13 = f32[1,50,50]{1,2,0:T(8,128)S(1)} custom-call(f32[1,50,50]{2,1,0:T(8,128)S(1)} %fusion.56), custom_call_target="InvertDiagBlocksLowerTriangular" | custom-call | tf_op jit(solution)/shard_map/triangular_solve/custom-call.2 | solution.py:17
  175.6 0.2 convolution_bitcast_fusion.9
  175.8 0.2 fusion.16
  176.0 0.1 maximum_bitcast_fusion.1
  176.0 0.3 fusion.19
  176.3 0.0 copy-start.7
  176.4 0.3 fusion.10
  176.6 12.5 %all_to_all.33 = bf16[16,8,3,128]{3,1,2,0:T(8,128)(2,1)S(1)} all-to-all(bf16[16,8,3,128]{3,1,2,0:T(8,128)(2,1)S(1)} %copy.63), channel_id=1, replica_groups=mesh['fluid'=16,'solid'=2] {'fluid'}, dimensions={0} | all-to-all | bytes 196608 | tf_op jit(solution)/shard_map/all_to_all | solution.py:65
  189.1 0.2 convolution_convert_fusion.3
  189.3 0.6 convolution_multiply_fusion
  190.0 0.7 copy.66
  (28 shorter events, 0.3 us)
Async XLA Ops:
  0.6 30.3 %copy-start = (bf16[64,128,128]{2,1,0:T(8,128)(2,1)S(1)}, bf16[64,128,128]{2,1,0:T(8,128)(2,1)}, u32[]{:S(2)}) copy-start(bf16[64,128,128]{2,1,0:T(8,128)(2,1)} %param.17) | copy-start | bytes 6291460
  19.8 10.9 %all-to-all-start.1 = ((bf16[16,8,3,128]{3,1,2,0:T(8,128)(2,1)}), bf16[16,8,3,128]{3,1,2,0:T(8,128)(2,1)S(1)}, u32[]{:S(2)}, u32[]{:S(2)}) async-start(bf16[16,8,3,128]{3,1,2,0:T(8,128)(2,1)} %copy.39), calls=%async_computation.1 | async-start | bytes 196608 | tf_op jit(solution)/shard_map/all_to_all | solution.py:65
  30.9 7.3 %copy-start.1 = (f32[50,1,4,3,128]{4,2,3,1,0:T(4,128)S(1)}, f32[50,1,4,3,128]{4,2,3,1,0:T(4,128)}, u32[]{:S(2)}) copy-start(f32[50,1,4,3,128]{4,2,3,1,0:T(4,128)} %param.23) | copy-start | bytes 921604
  30.9 16.3 %copy-start.5 = (f32[1,4,3,128]{3,1,2,0:T(4,128)S(1)}, f32[1,4,3,128]{3,1,2,0:T(4,128)}, u32[]{:S(2)}) copy-start(f32[1,4,3,128]{3,1,2,0:T(4,128)} %param.21) | copy-start | bytes 18436
  30.9 16.3 %copy-start.6 = (f32[1,4,3,128]{3,1,2,0:T(4,128)S(1)}, f32[1,4,3,128]{3,1,2,0:T(4,128)}, u32[]{:S(2)}) copy-start(f32[1,4,3,128]{3,1,2,0:T(4,128)} %param.22) | copy-start | bytes 18436
  33.6 63.4 %copy-start.2 = (f32[50,1,4,3,128]{4,2,3,1,0:T(4,128)S(1)}, f32[50,1,4,3,128]{4,2,3,1,0:T(4,128)}, u32[]{:S(2)}) copy-start(f32[50,1,4,3,128]{4,2,3,1,0:T(4,128)} %param.24) | copy-start | bytes 921604
  33.6 76.7 %copy-start.3 = (f32[64,3,128]{2,0,1:T(8,128)S(1)}, f32[64,3,128]{2,0,1:T(8,128)}, u32[]{:S(2)}) copy-start(f32[64,3,128]{2,0,1:T(8,128)} %param.15) | copy-start | bytes 294916
  33.6 76.7 %copy-start.4 = (f32[64,3,128]{2,0,1:T(8,128)S(1)}, f32[64,3,128]{2,0,1:T(8,128)}, u32[]{:S(2)}) copy-start(f32[64,3,128]{2,0,1:T(8,128)} %param.16) | copy-start | bytes 294916
  34.7 12.5 %all-to-all-start.2 = ((f32[16,8,3,128]{3,1,2,0:T(8,128)}), f32[16,8,3,128]{3,1,2,0:T(8,128)S(1)}, u32[]{:S(2)}, u32[]{:S(2)}) async-start(f32[16,8,3,128]{3,1,2,0:T(8,128)} %copy.45), calls=%async_computation.2 | async-start | bytes 393216 | tf_op jit(solution)/shard_map/all_to_all | solution.py:98
  113.2 12.5 %all-to-all-start.4 = ((f32[16,8,3,128]{3,1,2,0:T(8,128)}), f32[16,8,3,128]{3,1,2,0:T(8,128)S(1)}, u32[]{:S(2)}, u32[]{:S(2)}) async-start(f32[16,8,3,128]{3,1,2,0:T(8,128)} %copy.57), calls=%async_computation.4 | async-start | bytes 393216 | tf_op jit(solution)/shard_map/all_to_all | solution.py:98
  176.3 14.3 %copy-start.7 = (f32[1,4,3,128]{3,1,2,0:T(4,128)}, f32[1,4,3,128]{3,1,2,0:T(4,128)S(1)}, u32[]{:S(2)}) copy-start(f32[1,4,3,128]{3,1,2,0:T(4,128)S(1)} %copy_add_fusion) | copy-start | bytes 18436
where the time goes:
time: 192 us; the launch traced here: 191 us
  blocking collectives  114 us (59%)
  other arithmetic  24.1 us (13%)
  waiting for transfers between devices  24 us (12%)
  matrix products  11 us (6%)
  starting transfers between devices  10.5 us (5%)
  local copies, waits for them, and re-layouts  3.73 us (2%)
  between operations  2.92 us (2%)
    psum x2, blocking collectives, full_sums(): return lax.psum((gram_local, right_local), ('fluid', 'solid'))  75.8 us
    all_to_all x2, blocking collectives, to_fluid(): lax.all_to_all(chosen.reshape(fluid_size, capacity, 3, struct_width), 'fl...  24.9 us
    all_to_all x2, waiting for transfers between devices, body(): lax.all_to_all(buffer.reshape(fluid_size, capacity, 3, struct_width), 'fl...  17.3 us
    all_to_all x1, blocking collectives, body(): lax.all_to_all(sent_ids.reshape(fluid_size, capacity), 'fluid', split_axi...  13.6 us
    another operation x6, other arithmetic, solve_small(): jnp.linalg.cholesky(gram_matrix + ridge * jnp.eye(order, dtype=gram_matri...  10.5 us
    another operation x4, other arithmetic, solve_small(): lax.linalg.triangular_solve(factor, halfway, left_side=True, lower=True,...  8.96 us
    all_to_all x2, starting transfers between devices, body(): lax.all_to_all(buffer.reshape(fluid_size, capacity, 3, struct_width), 'fl...  7.04 us
    all_to_all x1, waiting for transfers between devices, to_fluid(): lax.all_to_all(chosen.reshape(fluid_size, capacity, 3, struct_width), 'fl...  6.69 us
  transfers between devices with their start and end apart: 3, of which 3 were waited for; matrix products, arithmetic and copies ran while one was open for 0% of the time, Pallas kernels for 0%

commit v1 on v0

v1 whole, which is shorter than its diff:
```python
import functools

import jax
import jax.numpy as jnp
from jax import lax
from jax.experimental import pallas as pl
from jax.experimental.pallas import tpu as pltpu
from jax.sharding import PartitionSpec as P

ridge_share = 0.01
MESH = pl.DeviceIdType.MESH
HIGH = lax.Precision.HIGHEST
F32 = jnp.float32
BF16 = jnp.bfloat16
NT = (((1,), (1,)), ((), ()))
HALF = 64
FORCE_TYPE = F32


def eliminate(m, order):
    rows = lax.broadcasted_iota(jnp.int32, m.shape, 0)
    for k in range(order):
        col = jnp.broadcast_to(m[:, k : k + 1], m.shape)
        row = m[k : k + 1, :] / col[k : k + 1, :]
        m = jnp.where(rows == k, row, m - col * row)
    return m


def kernel(
    nf, ns, dims,
    load_hbm, stiff_hbm, map_hbm, live, dest, local, comp, start, hist_hbm, upd_hbm,
    disp, fluid_out,
    mapping, loads, stiffs, hist, upd, comp16, x16,
    onehot, onehot_t, picked, contrib, u_out,
    xg, fs, fr, bg, gs, gr, gf,
    in_sems, out_sems, x_send, x_recv, f_send, f_recv, b_send, b_recv, g_send, g_recv,
):
    blocks, sub, order, iters = dims
    nd = nf * ns
    groups = blocks // 8
    slot = 4 * sub
    owners = HALF // 8
    fi = lax.axis_index("fluid")
    si = lax.axis_index("solid")
    me = fi * ns + si

    copies = [pltpu.make_async_copy(map_hbm, mapping, in_sems.at[0])]
    for c in range(3):
        copies.append(pltpu.make_async_copy(load_hbm.at[:, c], loads.at[c], in_sems.at[1 + c]))
        copies.append(pltpu.make_async_copy(stiff_hbm.at[:, c], stiffs.at[c], in_sems.at[4 + c]))
    hist_copies = []
    upd_copies = []
    for t in range(sub):
        for c in range(3):
            k = 3 * t + c
            hist_copies.append(
                pltpu.make_async_copy(
                    hist_hbm.at[:, 0, t, c], hist.at[k, pl.ds(0, order)], in_sems.at[7 + k]
                )
            )
            upd_copies.append(
                pltpu.make_async_copy(
                    upd_hbm.at[:, 0, t, c], upd.at[k, pl.ds(0, order)], in_sems.at[7 + 3 * sub + k]
                )
            )
    for copy in hist_copies + copies + upd_copies:
        copy.start()

    barrier = pltpu.get_barrier_semaphore()

    def greet(o, carry):
        p = lax.rem(me + o, nd)
        pl.semaphore_signal(barrier, inc=1, device_id=(p // ns, lax.rem(p, ns)), device_id_type=MESH)
        return carry

    lax.fori_loop(1, nd, greet, 0)

    comp16[...] = jnp.zeros_like(comp16)
    x16[...] = jnp.zeros_like(x16)
    for t in range(sub):
        comp16[4 * t : 4 * t + 3] = comp[0, t]
        x16[4 * t : 4 * t + 3] = start[0, t]
    for k in range(3 * sub):
        hist[k, order:] = jnp.zeros((HALF - order, 128), F32)
        upd[k, order:] = jnp.zeros((HALF - order, 128), F32)

    x = x16[...]
    xg[0, fi] = x.astype(BF16)

    eye = lax.broadcasted_iota(jnp.int32, (blocks, blocks), 0) == lax.broadcasted_iota(
        jnp.int32, (blocks, blocks), 1
    )
    local_col = jnp.sum(
        jnp.where(eye, jnp.broadcast_to(local[...].astype(F32), (blocks, blocks)), 0.0), axis=1, keepdims=True
    )
    row_id = lax.broadcasted_iota(jnp.int32, (blocks, 1), 0)
    first = dest[...].astype(F32) * slot + local_col * 4.0
    first = jnp.where(row_id < live[0], first, -8.0)
    parts = []
    for g in range(groups):
        one = first[8 * g : 8 * g + 8]
        parts += [one, one + 1.0, one + 2.0, jnp.full((8, 1), -8.0, F32)]
    target = jnp.concatenate(parts, axis=0)
    n_rows = 4 * blocks
    n_slots = nf * slot
    slot_id = lax.broadcasted_iota(jnp.int32, (n_rows, n_slots), 1).astype(F32)
    onehot[...] = jnp.where(slot_id == target, 1.0, 0.0).astype(BF16)
    diag = lax.broadcasted_iota(jnp.int32, (n_rows, n_rows), 0) == lax.broadcasted_iota(
        jnp.int32, (n_rows, n_rows), 1
    )
    target_row = jnp.sum(jnp.where(diag, jnp.broadcast_to(target, (n_rows, n_rows)), 0.0), axis=0, keepdims=True)
    slot_col = lax.broadcasted_iota(jnp.int32, (n_slots, n_rows), 0).astype(F32)
    onehot_t[...] = jnp.where(slot_col == target_row, 1.0, 0.0).astype(BF16)

    pl.semaphore_wait(barrier, nd - 1)

    def send_x(phase):
        def step(o, carry):
            p = lax.rem(fi + o, nf)
            pltpu.make_async_remote_copy(
                src_ref=xg.at[phase, fi], dst_ref=xg.at[phase, fi],
                send_sem=x_send.at[phase], recv_sem=x_recv.at[phase],
                device_id=(p, si), device_id_type=MESH,
            ).start()
            return carry

        lax.fori_loop(1, nf, step, 0)

    def wait_bytes(ref, sem):
        pltpu.make_async_copy(ref, ref, sem).wait()

    def send_f(phase):
        def step(o, carry):
            p = lax.rem(fi + o, nf)
            pltpu.make_async_remote_copy(
                src_ref=fs.at[phase, p], dst_ref=fr.at[phase, fi],
                send_sem=f_send.at[phase], recv_sem=f_recv.at[phase],
                device_id=(p, si), device_id_type=MESH,
            ).start()
            return carry

        lax.fori_loop(1, nf, step, 0)

    def send_all(ref, send_sem, recv_sem):
        def step(o, carry):
            p = lax.rem(me + o, nd)
            pltpu.make_async_remote_copy(
                src_ref=ref, dst_ref=ref, send_sem=send_sem, recv_sem=recv_sem,
                device_id=(p // ns, lax.rem(p, ns)), device_id_type=MESH,
            ).start()
            return carry

        lax.fori_loop(1, nd, step, 0)

    send_x(0)

    for copy in hist_copies:
        copy.wait()
    gram = jnp.zeros((HALF, HALF), F32)
    for k in range(3 * sub):
        v = hist[k]
        gram = gram + lax.dot_general(v, v, NT, precision=HIGH, preferred_element_type=F32)
    gram = jnp.concatenate([gram, jnp.zeros((HALF, 128 - HALF), F32)], axis=1)
    for o in range(owners):
        gs[o] = gram[8 * o : 8 * o + 8]
    for o in range(owners):
        @pl.when(me == o)
        def _():
            gr[me] = gs[o]

        @pl.when(me != o)
        def _():
            pltpu.make_async_remote_copy(
                src_ref=gs.at[o], dst_ref=gr.at[me], send_sem=g_send.at[0], recv_sem=g_recv.at[0],
                device_id=(o // ns, o % ns), device_id_type=MESH,
            ).start()

    mod8 = lax.rem(lax.broadcasted_iota(jnp.int32, (32, 128), 0), 8)

    def pick(phase):
        wait_bytes(xg.at[phase, pl.ds(0, nf - 1)], x_recv.at[phase])
        x_all = xg[phase].reshape(n_slots, 128)
        picked[...] = jnp.dot(onehot[...], x_all, preferred_element_type=F32)

    def to_fluid(g):
        rows = picked[32 * g : 32 * g + 32]
        lhs = jnp.concatenate([jnp.where(mod8 == i, rows, 0.0).astype(BF16) for i in range(8)], axis=1)
        return jnp.dot(lhs, mapping[8 * g : 8 * g + 8].reshape(8 * 128, 128), preferred_element_type=F32)

    def to_solid(g, u):
        force = []
        for c in range(3):
            span = slice(8 * g, 8 * g + 8)
            force.append(loads[c, span] - stiffs[c, span] * u[8 * c : 8 * c + 8])
        force = jnp.concatenate(force + [jnp.zeros((8, 128), F32)], axis=0)
        total = jnp.zeros((32, 128), F32)
        for i in range(8):
            total = total + lax.dot_general(
                jnp.where(mod8 == i, force, 0.0).astype(BF16), mapping[8 * g + i], NT, preferred_element_type=F32
            )
        return total

    resid = image = None
    inverse = gram_all = None
    lanes = lax.broadcasted_iota(jnp.int32, (HALF, 128), 1)
    rows = lax.broadcasted_iota(jnp.int32, (HALF, 128), 0)
    for it in range(iters):
        pick(it)
        if it == 0:
            for copy in copies:
                copy.wait()
        for g in range(groups):
            contrib[32 * g : 32 * g + 32] = to_solid(g, to_fluid(g))
        part = contrib[...]
        high = part.astype(BF16)
        low = (part - high.astype(F32)).astype(BF16)
        total = jnp.dot(onehot_t[...], high, preferred_element_type=F32) + jnp.dot(
            onehot_t[...], low, preferred_element_type=F32
        )
        fs[it] = total.reshape(nf, slot, 128).astype(FORCE_TYPE)
        fr[it, fi] = fs[it, fi]
        send_f(it)

        if it == 0:
            @pl.when(me < owners)
            def _():
                wait_bytes(gr.at[pl.ds(0, nd - 1)], g_recv.at[0])
                gf[me] = jnp.sum(gr[...], axis=0)
                send_all(gf.at[me], g_send.at[1], g_recv.at[1])

        wait_bytes(fr.at[it, pl.ds(0, nf - 1)], f_recv.at[it])
        new_image = comp16[...] * jnp.sum(fr[it].astype(F32), axis=0)
        new_resid = new_image - x
        acc_r = jnp.zeros((HALF, 128), F32)
        acc_d = jnp.zeros((HALF, 128), F32)
        if it == 0:
            for k in range(3 * sub):
                at = 4 * (k // 3) + k % 3
                acc_r = acc_r + hist[k] * new_resid[at : at + 1]
        else:
            newest = new_resid - resid
            shift = new_image - image
            for k in range(3 * sub):
                at = 4 * (k // 3) + k % 3
                hist[k, order : order + 1] = newest[at : at + 1]
                upd[k, order : order + 1] = shift[at : at + 1]
            for k in range(3 * sub):
                at = 4 * (k // 3) + k % 3
                acc_r = acc_r + hist[k] * new_resid[at : at + 1]
                acc_d = acc_d + hist[k] * newest[at : at + 1]
        resid, image = new_resid, new_image
        acc = jnp.concatenate([acc_d, acc_r], axis=0)
        sums = lax.dot_general(jnp.ones((8, 128), F32), acc, NT, precision=HIGH, preferred_element_type=F32)
        bg[it, me] = sums[0:1]
        send_all(bg.at[it, me], b_send.at[it], b_recv.at[it])

        if it == 0:
            @pl.when(me < owners)
            def _():
                wait_bytes(gf.at[pl.ds(0, owners - 1)], g_recv.at[1])

            @pl.when(me >= owners)
            def _():
                wait_bytes(gf, g_recv.at[1])

            gram_all = gf[...].reshape(HALF, 128)
            trace = jnp.sum(jnp.where(lanes == rows, gram_all, 0.0), keepdims=True)
            ridge = ridge_share * trace / order
            inside = (rows < order)
            matrix = gram_all + jnp.where(lanes == rows, jnp.where(inside, ridge, 1.0), 0.0)
            matrix = matrix + jnp.where(lanes == rows + HALF, 1.0, 0.0)
            inverse = eliminate(matrix, order)
            for copy in upd_copies:
                copy.wait()

        wait_bytes(bg.at[it, pl.ds(0, nd - 1)], b_recv.at[it])
        sums = jnp.sum(bg[it], axis=0)
        if it == 0:
            coef = -jnp.sum(jnp.where(lanes >= HALF, inverse * sums, 0.0), axis=1, keepdims=True)
        else:
            column = jnp.sum(jnp.where(lanes == rows, sums, 0.0), axis=1, keepdims=True)
            right = jnp.sum(jnp.where(lanes == rows + HALF, sums, 0.0), axis=1, keepdims=True)
            old = (rows >= 1) & (rows < order) & (lanes >= 1) & (lanes < order)
            matrix = jnp.where(old, gram_all, 0.0)
            matrix = jnp.where((rows == order) & (lanes >= 1) & (lanes <= order), sums, matrix)
            matrix = jnp.where((lanes == order) & (rows >= 1) & (rows < order), column, matrix)
            trace = jnp.sum(jnp.where(lanes == rows, matrix, 0.0), keepdims=True)
            ridge = ridge_share * trace / order
            inside = (rows >= 1) & (rows <= order)
            matrix = matrix + jnp.where(lanes == rows, jnp.where(inside, ridge, 1.0), 0.0)
            matrix = jnp.where(lanes == HALF, jnp.where(inside, right, 0.0), matrix)
            solved = eliminate(matrix, order + 1)
            coef = -solved[:, HALF : HALF + 1]
        pieces = []
        for t in range(sub):
            for c in range(3):
                pieces.append(jnp.sum(upd[3 * t + c] * coef, axis=0, keepdims=True))
            pieces.append(jnp.zeros((1, 128), F32))
        x = image + jnp.concatenate(pieces, axis=0)
        xg[it + 1, fi] = x.astype(BF16)
        send_x(it + 1)

    for t in range(sub):
        disp[0, t] = x[4 * t : 4 * t + 3]

    pick(iters)
    for g in range(groups):
        u = to_fluid(g)
        for c in range(3):
            u_out[c, 8 * g : 8 * g + 8] = u[8 * c : 8 * c + 8]
    out_copies = [
        pltpu.make_async_copy(u_out.at[c], fluid_out.at[:, c], out_sems.at[c]) for c in range(3)
    ]
    for copy in out_copies:
        copy.start()

    for phase in range(iters + 1):
        wait_bytes(xg.at[phase, pl.ds(0, nf - 1)], x_send.at[phase])
    for phase in range(iters):
        wait_bytes(fr.at[phase, pl.ds(0, nf - 1)], f_send.at[phase])
        wait_bytes(bg.at[phase, pl.ds(0, nd - 1)], b_send.at[phase])
    @pl.when(me >= owners)
    def _():
        wait_bytes(gs, g_send.at[0])

    @pl.when(me < owners)
    def _():
        wait_bytes(gs.at[pl.ds(0, owners - 1)], g_send.at[0])
        wait_bytes(gr.at[pl.ds(0, nd - 1)], g_send.at[1])

    for copy in out_copies:
        copy.wait()


def body(load, stiff, mapping, live, dest, local, comp, start, hist, upd, *, nf, ns):
    blocks = mapping.shape[0]
    sub = comp.shape[1]
    order = hist.shape[0]
    iters = 2
    nd = nf * ns
    slot = 4 * sub
    owners = HALF // 8
    vmem = pl.BlockSpec(memory_space=pltpu.VMEM)
    smem = pl.BlockSpec(memory_space=pltpu.SMEM)
    hbm = pl.BlockSpec(memory_space=pl.ANY)
    dma = pltpu.SemaphoreType.DMA
    return pl.pallas_call(
        functools.partial(kernel, nf, ns, (blocks, sub, order, iters)),
        out_shape=(
            jax.ShapeDtypeStruct(comp.shape, F32),
            jax.ShapeDtypeStruct(load.shape, F32),
        ),
        in_specs=[hbm, hbm, hbm, smem, vmem, vmem, vmem, vmem, hbm, hbm],
        out_specs=(vmem, hbm),
        scratch_shapes=[
            pltpu.VMEM(mapping.shape, BF16),
            pltpu.VMEM((3, blocks, 128), F32),
            pltpu.VMEM((3, blocks, 128), F32),
            pltpu.VMEM((3 * sub, HALF, 128), F32),
            pltpu.VMEM((3 * sub, HALF, 128), F32),
            pltpu.VMEM((slot, 128), F32),
            pltpu.VMEM((slot, 128), F32),
            pltpu.VMEM((4 * blocks, nf * slot), BF16),
            pltpu.VMEM((nf * slot, 4 * blocks), BF16),
            pltpu.VMEM((4 * blocks, 128), F32),
            pltpu.VMEM((4 * blocks, 128), F32),
            pltpu.VMEM((3, blocks, 128), F32),
            pltpu.VMEM((iters + 1, nf, slot, 128), BF16),
            pltpu.VMEM((iters, nf, slot, 128), FORCE_TYPE),
            pltpu.VMEM((iters, nf, slot, 128), FORCE_TYPE),
            pltpu.VMEM((iters, nd, 1, 128), F32),
            pltpu.VMEM((owners, 8, 128), F32),
            pltpu.VMEM((nd, 8, 128), F32),
            pltpu.VMEM((owners, 8, 128), F32),
            dma((7 + 6 * sub,)),
            dma((3,)),
            dma((iters + 1,)),
            dma((iters + 1,)),
            dma((iters,)),
            dma((iters,)),
            dma((iters,)),
            dma((iters,)),
            dma((2,)),
            dma((2,)),
        ],
        compiler_params=pltpu.CompilerParams(collective_id=0, has_side_effects=True),
    )(load, stiff, mapping, live, dest, local.reshape(1, blocks), comp, start, hist, upd)


def solution(mesh):
    in_specs = (
        P(("fluid", "solid"), None, None),
        P(("fluid", "solid"), None, None),
        P(("fluid", "solid"), None, None),
        P(("fluid", "solid")),
        P(("fluid", "solid"), None),
        P(("fluid", "solid")),
        P("solid", "fluid", None, None),
        P("solid", "fluid", None, None),
        P(None, "solid", "fluid", None, None),
        P(None, "solid", "fluid", None, None),
    )
    out_specs = (P("solid", "fluid", None, None), P(("fluid", "solid"), None, None))
    inner = functools.partial(body, nf=mesh.shape["fluid"], ns=mesh.shape["solid"])
    return jax.shard_map(inner, mesh=mesh, in_specs=in_specs, out_specs=out_specs, check_vma=False)
```

time: 192 us -> 68.4 us (0.36)
  blocking collectives: 114 us -> 0 us
  Pallas kernels: 0 us -> 53 us
  other arithmetic: 24.1 us -> 0 us
  waiting for transfers between devices: 24 us -> 0 us
  matrix products: 11 us -> 0 us
  starting transfers between devices: 10.5 us -> 0 us
  local copies, waits for them, and re-layouts: 3.73 us -> 13.6 us
    psum x2 -> x0, blocking collectives: 75.8 us -> none  [full_sums(): return lax.psum((gram_local, right_local), ('fluid', 'solid'))]
    pallas_call x0 -> x1, Pallas kernels: none -> 53 us  [body(): pl.pallas_call(functools.partial(kernel, nf, ns, (blocks, sub, order, ite...]
    all_to_all x3 -> x0, blocking collectives: 38.5 us -> none  [the longest x2 24.9 us: to_fluid(): lax.all_to_all(chosen.reshape(fluid_size, capacity, 3, struct_width), 'fl...]
    all_to_all x3 -> x0, waiting for transfers between devices: 24 us -> none  [the longest x2 17.3 us: body(): lax.all_to_all(buffer.reshape(fluid_size, capacity, 3, struct_width), 'fl...]
    another operation x13 -> x0, other arithmetic: 19.6 us -> none  [the longest x6 10.5 us: solve_small(): jnp.linalg.cholesky(gram_matrix + ridge * jnp.eye(order, dtype=gram_matri...]
    all_to_all x3 -> x0, starting transfers between devices: 10.5 us -> none  [the longest x2 7.04 us: body(): lax.all_to_all(buffer.reshape(fluid_size, capacity, 3, struct_width), 'fl...]
    dot_general x19 -> x0, matrix products: 10.4 us -> none  [the longest x2 4.43 us: body(): jnp.einsum('bjn,bcn->bcj', mapping, fluid_force, preferred_element_type=j...]
    unnamed x18 -> x7, local copies, waits for them, and re-layouts: 0.73 us -> 10.8 us
  transfers between devices with their start and end apart: 3 -> 0, of which waited for: 3 -> 0; matrix products, arithmetic and copies ran while one was open for 0% -> 0% of each run, Pallas kernels for 0% -> 0%
where the time goes in v1:
time: 68.4 us; the launch traced here: 68 us
  Pallas kernels  53 us (77%)
  local copies, waits for them, and re-layouts  13.6 us (20%)
  between operations  1.29 us (2%)
    pallas_call x1, Pallas kernels, body(): pl.pallas_call(functools.partial(kernel, nf, ns, (blocks, sub, order, ite...  53 us
    unnamed x7, local copies, waits for them, and re-layouts  10.8 us
    pallas_call x2, local copies, waits for them, and re-layouts, body(): pl.pallas_call(functools.partial(kernel, nf, ns, (blocks, sub, order, ite...  2.84 us

profile of v1, /device:TPU:0, one launch (start us, length us, event | category | flops | bytes accessed | tf_op | source)
XLA Modules:
  0.0 68.0 jit_solution(1004355011946251409)
XLA Ops:
  1.3 1.3 %copy.15.comp = f32[1,4,3,128]{3,2,1,0:T(4,128)} copy(f32[1,4,3,128]{3,1,2,0:T(4,128)} %param.16) | data formatting | bytes 12288 | tf_op args[6]
  2.6 1.3 %copy.16.start = f32[1,4,3,128]{3,2,1,0:T(4,128)} copy(f32[1,4,3,128]{3,1,2,0:T(4,128)} %param.17) | data formatting | bytes 12288 | tf_op args[7]
  3.9 1.4 %copy.14.dest = s32[64,1]{1,0:T(8,128)} copy(s32[64,1]{0,1:T(1,128)} %param.14) | data formatting | bytes 512 | tf_op args[4]
  5.2 1.6 %copy.12.load_hbm = f32[64,3,128]{2,1,0:T(4,128)} copy(f32[64,3,128]{2,0,1:T(8,128)} %param.10) | data formatting | bytes 196608 | tf_op args[0]
  6.8 1.6 %copy.13.stiff_hbm = f32[64,3,128]{2,1,0:T(4,128)} copy(f32[64,3,128]{2,0,1:T(8,128)} %param.11) | data formatting | bytes 196608 | tf_op args[1]
  8.4 1.8 %copy.17.hist_hbm = f32[50,1,4,3,128]{4,3,2,1,0:T(4,128)} copy(f32[50,1,4,3,128]{4,2,3,1,0:T(4,128)} %param.18) | data formatting | bytes 614400 | tf_op args[8]
  10.3 1.8 %copy.18.upd_hbm = f32[50,1,4,3,128]{4,3,2,1,0:T(4,128)} copy(f32[50,1,4,3,128]{4,2,3,1,0:T(4,128)} %param.19) | data formatting | bytes 614400 | tf_op args[9]
  12.1 53.0 %shard_map.113 = (f32[1,4,3,128]{3,2,1,0:T(4,128)}, f32[64,3,128]{2,1,0:T(4,128)}) custom-call(f32[64,3,128]{2,1,0:T(4,128)} %copy.12.load_hbm, f32[64,3,128]{2,1,0:T(4,128)} %copy.13.stiff_hbm, bf16[64,128,128]{2,1,0:T(8,128)(2,1)} %map_hbm.1, s32[1]{0:T(128)S(6)} %copy.21.live, s32[64,1]{1,0:T(8,128)} %copy.14.dest, s32[1,64]{1,0:T(1,128)} %bitcast.1, ...), custom_call_target="tpu_custom_call" | custom-call | tf_op jit(solution)/shard_map/pallas_call | solution.py:347
  65.1 1.3 %copy.19 = f32[1,4,3,128]{3,1,2,0:T(4,128)} copy(f32[1,4,3,128]{3,2,1,0:T(4,128)} %get-tuple-element.2) | data formatting | bytes 12288 | tf_op jit(solution)/shard_map/pallas_call | solution.py:347
  66.4 1.6 %copy.20 = f32[64,3,128]{2,0,1:T(8,128)} copy(f32[64,3,128]{2,1,0:T(4,128)} %get-tuple-element.3) | data formatting | bytes 196608 | tf_op jit(solution)/shard_map/pallas_call | solution.py:347

commit v2 on v1

--- a/solution.py
+++ b/solution.py
@@ -14,92 +14,139 @@
 BF16 = jnp.bfloat16
 NT = (((1,), (1,)), ((), ()))
 HALF = 64
-FORCE_TYPE = F32
-
-
-def eliminate(m, order):
+FORCE_TYPE = BF16
+
+
+def eliminate(m, first, last):
     rows = lax.broadcasted_iota(jnp.int32, m.shape, 0)
-    for k in range(order):
-        col = jnp.broadcast_to(m[:, k : k + 1], m.shape)
-        row = m[k : k + 1, :] / col[k : k + 1, :]
-        m = jnp.where(rows == k, row, m - col * row)
+    for k in range(first, last, 2):
+        a = jnp.broadcast_to(m[:, k : k + 1], m.shape)
+        b = jnp.broadcast_to(m[:, k + 1 : k + 2], m.shape)
+        p, q = a[k : k + 1], b[k : k + 1]
+        u, v = a[k + 1 : k + 2], b[k + 1 : k + 2]
+        over = 1.0 / (p * v - q * u)
+        top, low = m[k : k + 1], m[k + 1 : k + 2]
+        new_top = (v * top - q * low) * over
+        new_low = (p * low - u * top) * over
+        m = m - a * new_top - b * new_low
+        m = jnp.where(rows == k, new_top, jnp.where(rows == k + 1, new_low, m))
     return m
+
+
+def send_order(n):
+    return sorted(range(1, n), key=lambda o: -min(o, n - o))
+
+
+def loop(n, step):
+    if n <= 16:
+        for o in send_order(n):
+            step(o)
+    else:
+        def one(o, carry):
+            step(o)
+            return carry
+
+        lax.fori_loop(1, n, one, 0)
+
+
+def wrap(a, n):
+    return jnp.where(a >= n, a - n, a)
 
 
 def kernel(
     nf, ns, dims,
-    load_hbm, stiff_hbm, map_hbm, live, dest, local, comp, start, hist_hbm, upd_hbm,
-    disp, fluid_out,
+    load_hbm, stiff_hbm, map_hbm, live_hbm, dest_hbm, local_hbm, comp_hbm, start_hbm, hist_hbm, upd_hbm,
+    disp, delta, fluid_out,
+    live, dest, local, comp, start,
     mapping, loads, stiffs, hist, upd, comp16, x16,
     onehot, onehot_t, picked, contrib, u_out,
     xg, fs, fr, bg, gs, gr, gf,
-    in_sems, out_sems, x_send, x_recv, f_send, f_recv, b_send, b_recv, g_send, g_recv,
+    small_sems, in_sems, out_sems, x_send, x_recv, f_send, f_recv, b_send, b_recv, g_send, g_recv,
 ):
     blocks, sub, order, iters = dims
     nd = nf * ns
     groups = blocks // 8
-    slot = 4 * sub
+    slot = -(-3 * sub // 16) * 16
     owners = HALF // 8
+    used = 3 * sub
+    tall = -(-(order + 2) // 8) * 8
     fi = lax.axis_index("fluid")
     si = lax.axis_index("solid")
     me = fi * ns + si
 
+    def everyone(step):
+        def with_all(o):
+            for k in range(ns):
+                step(wrap(fi + o, nf), wrap(si + k, ns))
+
+        loop(nf, with_all)
+        for k in range(1, ns):
+            step(fi, wrap(si + k, ns))
+
+    barrier = pltpu.get_barrier_semaphore()
+    xg[:, :, used:] = jnp.zeros((iters + 1, nf, slot - used, 128), BF16)
+    fr[:, :, used:] = jnp.zeros((iters, nf, slot - used, 128), FORCE_TYPE)
+
+    def greet(p, q):
+        pl.semaphore_signal(barrier, inc=1, device_id=(p, q), device_id_type=MESH)
+
+    small = [
+        pltpu.make_async_copy(ref, to, small_sems.at[i])
+        for i, (ref, to) in enumerate(
+            [(live_hbm, live), (dest_hbm, dest), (local_hbm, local), (comp_hbm, comp), (start_hbm, start)]
+        )
+    ]
+    for copy in small:
+        copy.start()
+    everyone(greet)
+
     copies = [pltpu.make_async_copy(map_hbm, mapping, in_sems.at[0])]
     for c in range(3):
-        copies.append(pltpu.make_async_copy(load_hbm.at[:, c], loads.at[c], in_sems.at[1 + c]))
-        copies.append(pltpu.make_async_copy(stiff_hbm.at[:, c], stiffs.at[c], in_sems.at[4 + c]))
+        copies.append(pltpu.make_async_copy(load_hbm.at[c], loads.at[c], in_sems.at[1 + c]))
+        copies.append(pltpu.make_async_copy(stiff_hbm.at[c], stiffs.at[c], in_sems.at[4 + c]))
     hist_copies = []
     upd_copies = []
-    for t in range(sub):
-        for c in range(3):
-            k = 3 * t + c
+    for c in range(3):
+        for t in range(sub):
+            k = sub * c + t
             hist_copies.append(
                 pltpu.make_async_copy(
-                    hist_hbm.at[:, 0, t, c], hist.at[k, pl.ds(0, order)], in_sems.at[7 + k]
+                    hist_hbm.at[:, 0, c, t], hist.at[k, pl.ds(0, order)], in_sems.at[7 + k]
                 )
             )
             upd_copies.append(
                 pltpu.make_async_copy(
-                    upd_hbm.at[:, 0, t, c], upd.at[k, pl.ds(0, order)], in_sems.at[7 + 3 * sub + k]
+                    upd_hbm.at[:, 0, c, t], upd.at[k, pl.ds(0, order)], in_sems.at[7 + 3 * sub + k]
                 )
             )
     for copy in hist_copies + copies + upd_copies:
         copy.start()
 
-    barrier = pltpu.get_barrier_semaphore()
-
-    def greet(o, carry):
-        p = lax.rem(me + o, nd)
-        pl.semaphore_signal(barrier, inc=1, device_id=(p // ns, lax.rem(p, ns)), device_id_type=MESH)
-        return carry
-
-    lax.fori_loop(1, nd, greet, 0)
-
+    for copy in small:
+        copy.wait()
     comp16[...] = jnp.zeros_like(comp16)
     x16[...] = jnp.zeros_like(x16)
-    for t in range(sub):
-        comp16[4 * t : 4 * t + 3] = comp[0, t]
-        x16[4 * t : 4 * t + 3] = start[0, t]
+    for c in range(3):
+        comp16[sub * c : sub * c + sub] = comp[0, c]
+        x16[sub * c : sub * c + sub] = start[0, c]
     for k in range(3 * sub):
         hist[k, order:] = jnp.zeros((HALF - order, 128), F32)
         upd[k, order:] = jnp.zeros((HALF - order, 128), F32)
 
     x = x16[...]
-    xg[0, fi] = x.astype(BF16)
+    xg[0, fi, :used] = x[:used].astype(BF16)
 
     eye = lax.broadcasted_iota(jnp.int32, (blocks, blocks), 0) == lax.broadcasted_iota(
         jnp.int32, (blocks, blocks), 1
     )
-    local_col = jnp.sum(
-        jnp.where(eye, jnp.broadcast_to(local[...].astype(F32), (blocks, blocks)), 0.0), axis=1, keepdims=True
-    )
-    row_id = lax.broadcasted_iota(jnp.int32, (blocks, 1), 0)
-    first = dest[...].astype(F32) * slot + local_col * 4.0
-    first = jnp.where(row_id < live[0], first, -8.0)
+    base = dest[...].astype(F32) * slot + local[...].astype(F32)
+    column_id = lax.broadcasted_iota(jnp.int32, (1, blocks), 1)
+    base = jnp.where(column_id < live[...], base, -3.0 * slot)
+    first = jnp.sum(jnp.where(eye, jnp.broadcast_to(base, (blocks, blocks)), 0.0), axis=1, keepdims=True)
     parts = []
     for g in range(groups):
         one = first[8 * g : 8 * g + 8]
-        parts += [one, one + 1.0, one + 2.0, jnp.full((8, 1), -8.0, F32)]
+        parts += [one, one + sub, one + 2.0 * sub, jnp.full((8, 1), -1.0, F32)]
     target = jnp.concatenate(parts, axis=0)
     n_rows = 4 * blocks
     n_slots = nf * slot
@@ -112,45 +159,42 @@
     slot_col = lax.broadcasted_iota(jnp.int32, (n_slots, n_rows), 0).astype(F32)
     onehot_t[...] = jnp.where(slot_col == target_row, 1.0, 0.0).astype(BF16)
 
-    pl.semaphore_wait(barrier, nd - 1)
+    with jax.named_scope("wait_barrier"):
+        pl.semaphore_wait(barrier, nd - 1)
 
     def send_x(phase):
-        def step(o, carry):
-            p = lax.rem(fi + o, nf)
+        def step(o):
+            p = wrap(fi + o, nf)
             pltpu.make_async_remote_copy(
-                src_ref=xg.at[phase, fi], dst_ref=xg.at[phase, fi],
+                src_ref=xg.at[phase, fi, pl.ds(0, used)], dst_ref=xg.at[phase, fi, pl.ds(0, used)],
                 send_sem=x_send.at[phase], recv_sem=x_recv.at[phase],
                 device_id=(p, si), device_id_type=MESH,
             ).start()
-            return carry
-
-        lax.fori_loop(1, nf, step, 0)
+
+        loop(nf, step)
 
     def wait_bytes(ref, sem):
         pltpu.make_async_copy(ref, ref, sem).wait()
 
     def send_f(phase):
-        def step(o, carry):
-            p = lax.rem(fi + o, nf)
+        def step(o):
+            p = wrap(fi + o, nf)
             pltpu.make_async_remote_copy(
-                src_ref=fs.at[phase, p], dst_ref=fr.at[phase, fi],
+                src_ref=fs.at[phase, p, pl.ds(0, used)], dst_ref=fr.at[phase, fi, pl.ds(0, used)],
                 send_sem=f_send.at[phase], recv_sem=f_recv.at[phase],
                 device_id=(p, si), device_id_type=MESH,
             ).start()
-            return carry
-
-        lax.fori_loop(1, nf, step, 0)
+
+        loop(nf, step)
 
     def send_all(ref, send_sem, recv_sem):
-        def step(o, carry):
-            p = lax.rem(me + o, nd)
+        def step(p, q):
             pltpu.make_async_remote_copy(
                 src_ref=ref, dst_ref=ref, send_sem=send_sem, recv_sem=recv_sem,
-                device_id=(p // ns, lax.rem(p, ns)), device_id_type=MESH,
+                device_id=(p, q), device_id_type=MESH,
             ).start()
-            return carry
-
-        lax.fori_loop(1, nd, step, 0)
+
+        everyone(step)
 
     send_x(0)
 
@@ -178,7 +222,8 @@
     mod8 = lax.rem(lax.broadcasted_iota(jnp.int32, (32, 128), 0), 8)
 
     def pick(phase):
-        wait_bytes(xg.at[phase, pl.ds(0, nf - 1)], x_recv.at[phase])
+        with jax.named_scope("wait_x"):
+            wait_bytes(xg.at[phase, pl.ds(0, nf - 1), pl.ds(0, used)], x_recv.at[phase])
         x_all = xg[phase].reshape(n_slots, 128)
         picked[...] = jnp.dot(onehot[...], x_all, preferred_element_type=F32)
 
@@ -207,10 +252,12 @@
     for it in range(iters):
         pick(it)
         if it == 0:
-            for copy in copies:
-                copy.wait()
-        for g in range(groups):
-            contrib[32 * g : 32 * g + 32] = to_solid(g, to_fluid(g))
+            with jax.named_scope("wait_in"):
+                for copy in copies:
+                    copy.wait()
+        with jax.named_scope("blocks"):
+            for g in range(groups):
+                contrib[32 * g : 32 * g + 32] = to_solid(g, to_fluid(g))
         part = contrib[...]
         high = part.astype(BF16)
         low = (part - high.astype(F32)).astype(BF16)
@@ -218,7 +265,7 @@
             onehot_t[...], low, preferred_element_type=F32
         )
         fs[it] = total.reshape(nf, slot, 128).astype(FORCE_TYPE)
-        fr[it, fi] = fs[it, fi]
+        fr[it, fi, :used] = fs[it, fi, :used]
         send_f(it)
 
         if it == 0:
@@ -228,26 +275,24 @@
                 gf[me] = jnp.sum(gr[...], axis=0)
                 send_all(gf.at[me], g_send.at[1], g_recv.at[1])
 
-        wait_bytes(fr.at[it, pl.ds(0, nf - 1)], f_recv.at[it])
+        with jax.named_scope("wait_f"):
+            wait_bytes(fr.at[it, pl.ds(0, nf - 1), pl.ds(0, used)], f_recv.at[it])
         new_image = comp16[...] * jnp.sum(fr[it].astype(F32), axis=0)
         new_resid = new_image - x
         acc_r = jnp.zeros((HALF, 128), F32)
         acc_d = jnp.zeros((HALF, 128), F32)
         if it == 0:
             for k in range(3 * sub):
-                at = 4 * (k // 3) + k % 3
-                acc_r = acc_r + hist[k] * new_resid[at : at + 1]
+                acc_r = acc_r + hist[k] * new_resid[k : k + 1]
         else:
             newest = new_resid - resid
             shift = new_image - image
             for k in range(3 * sub):
-                at = 4 * (k // 3) + k % 3
-                hist[k, order : order + 1] = newest[at : at + 1]
-                upd[k, order : order + 1] = shift[at : at + 1]
+                hist[k, order : order + 1] = newest[k : k + 1]
+                upd[k, order : order + 1] = shift[k : k + 1]
             for k in range(3 * sub):
-                at = 4 * (k // 3) + k % 3
-                acc_r = acc_r + hist[k] * new_resid[at : at + 1]
-                acc_d = acc_d + hist[k] * newest[at : at + 1]
+                acc_r = acc_r + hist[k] * new_resid[k : k + 1]
+                acc_d = acc_d + hist[k] * newest[k : k + 1]
         resid, image = new_resid, new_image
         acc = jnp.concatenate([acc_d, acc_r], axis=0)
         sums = lax.dot_general(jnp.ones((8, 128), F32), acc, NT, precision=HIGH, preferred_element_type=F32)
@@ -269,14 +314,16 @@
             inside = (rows < order)
             matrix = gram_all + jnp.where(lanes == rows, jnp.where(inside, ridge, 1.0), 0.0)
             matrix = matrix + jnp.where(lanes == rows + HALF, 1.0, 0.0)
-            inverse = eliminate(matrix, order)
+            with jax.named_scope("solve1"):
+                inverse = eliminate(matrix[:tall], 0, order)
             for copy in upd_copies:
                 copy.wait()
 
-        wait_bytes(bg.at[it, pl.ds(0, nd - 1)], b_recv.at[it])
+        with jax.named_scope("wait_b"):
+            wait_bytes(bg.at[it, pl.ds(0, nd - 1)], b_recv.at[it])
         sums = jnp.sum(bg[it], axis=0)
         if it == 0:
-            coef = -jnp.sum(jnp.where(lanes >= HALF, inverse * sums, 0.0), axis=1, keepdims=True)
+            coef = -jnp.sum(jnp.where(lanes[:tall] >= HALF, inverse * sums, 0.0), axis=1, keepdims=True)
         else:
             column = jnp.sum(jnp.where(lanes == rows, sums, 0.0), axis=1, keepdims=True)
             right = jnp.sum(jnp.where(lanes == rows + HALF, sums, 0.0), axis=1, keepdims=True)
@@ -289,19 +336,21 @@
             inside = (rows >= 1) & (rows <= order)
             matrix = matrix + jnp.where(lanes == rows, jnp.where(inside, ridge, 1.0), 0.0)
             matrix = jnp.where(lanes == HALF, jnp.where(inside, right, 0.0), matrix)
-            solved = eliminate(matrix, order + 1)
+            with jax.named_scope("solve2"):
+                solved = eliminate(matrix[:tall], 1, order + 1)
             coef = -solved[:, HALF : HALF + 1]
         pieces = []
-        for t in range(sub):
-            for c in range(3):
-                pieces.append(jnp.sum(upd[3 * t + c] * coef, axis=0, keepdims=True))
-            pieces.append(jnp.zeros((1, 128), F32))
-        x = image + jnp.concatenate(pieces, axis=0)
-        xg[it + 1, fi] = x.astype(BF16)
+        for k in range(3 * sub):
+            pieces.append(jnp.sum(upd[k, :tall] * coef, axis=0, keepdims=True))
+        pieces.append(jnp.zeros((slot - 3 * sub, 128), F32))
+        change = jnp.concatenate(pieces, axis=0)
+        x = image + change
+        xg[it + 1, fi, :used] = x[:used].astype(BF16)
         send_x(it + 1)
 
-    for t in range(sub):
-        disp[0, t] = x[4 * t : 4 * t + 3]
+    for c in range(3):
+        disp[0, c] = image[sub * c : sub * c + sub]
+        delta[0, c] = change[sub * c : sub * c + sub]
 
     pick(iters)
     for g in range(groups):
@@ -309,15 +358,15 @@
         for c in range(3):
             u_out[c, 8 * g : 8 * g + 8] = u[8 * c : 8 * c + 8]
     out_copies = [
-        pltpu.make_async_copy(u_out.at[c], fluid_out.at[:, c], out_sems.at[c]) for c in range(3)
+        pltpu.make_async_copy(u_out.at[c], fluid_out.at[c], out_sems.at[c]) for c in range(3)
     ]
     for copy in out_copies:
         copy.start()
 
     for phase in range(iters + 1):
-        wait_bytes(xg.at[phase, pl.ds(0, nf - 1)], x_send.at[phase])
+        wait_bytes(xg.at[phase, pl.ds(0, nf - 1), pl.ds(0, used)], x_send.at[phase])
     for phase in range(iters):
-        wait_bytes(fr.at[phase, pl.ds(0, nf - 1)], f_send.at[phase])
+        wait_bytes(fr.at[phase, pl.ds(0, nf - 1), pl.ds(0, used)], f_send.at[phase])
         wait_bytes(bg.at[phase, pl.ds(0, nd - 1)], b_send.at[phase])
     @pl.when(me >= owners)
     def _():
@@ -338,21 +387,26 @@
     order = hist.shape[0]
     iters = 2
     nd = nf * ns
-    slot = 4 * sub
+    slot = -(-3 * sub // 16) * 16
     owners = HALF // 8
     vmem = pl.BlockSpec(memory_space=pltpu.VMEM)
-    smem = pl.BlockSpec(memory_space=pltpu.SMEM)
     hbm = pl.BlockSpec(memory_space=pl.ANY)
     dma = pltpu.SemaphoreType.DMA
-    return pl.pallas_call(
+    disp, delta, fluid = pl.pallas_call(
         functools.partial(kernel, nf, ns, (blocks, sub, order, iters)),
         out_shape=(
-            jax.ShapeDtypeStruct(comp.shape, F32),
-            jax.ShapeDtypeStruct(load.shape, F32),
+            jax.ShapeDtypeStruct((1, 3, sub, 128), F32),
+            jax.ShapeDtypeStruct((1, 3, sub, 128), F32),
+            jax.ShapeDtypeStruct((3, blocks, 128), F32),
         ),
-        in_specs=[hbm, hbm, hbm, smem, vmem, vmem, vmem, vmem, hbm, hbm],
-        out_specs=(vmem, hbm),
+        in_specs=[hbm] * 10,
+        out_specs=(vmem, vmem, vmem),
         scratch_shapes=[
+            pltpu.VMEM((1, 1), jnp.int32),
+            pltpu.VMEM((1, blocks), jnp.int32),
+            pltpu.VMEM((1, blocks), jnp.int32),
+            pltpu.VMEM((1, 3, sub, 128), F32),
+            pltpu.VMEM((1, 3, sub, 128), F32),
             pltpu.VMEM(mapping.shape, BF16),
             pltpu.VMEM((3, blocks, 128), F32),
             pltpu.VMEM((3, blocks, 128), F32),
@@ -372,6 +426,7 @@
             pltpu.VMEM((owners, 8, 128), F32),
             pltpu.VMEM((nd, 8, 128), F32),
             pltpu.VMEM((owners, 8, 128), F32),
+            dma((5,)),
             dma((7 + 6 * sub,)),
             dma((3,)),
             dma((iters + 1,)),
@@ -383,8 +438,15 @@
             dma((2,)),
             dma((2,)),
         ],
-        compiler_params=pltpu.CompilerParams(collective_id=0, has_side_effects=True),
-    )(load, stiff, mapping, live, dest, local.reshape(1, blocks), comp, start, hist, upd)
+        compiler_params=pltpu.CompilerParams(collective_id=0, has_side_effects=True, vmem_limit_bytes=63400000),
+    )(
+        load.transpose(1, 0, 2), stiff.transpose(1, 0, 2), mapping, live.reshape(1, 1),
+        dest.reshape(1, blocks), local.reshape(1, blocks),
+        comp.transpose(0, 2, 1, 3), start.transpose(0, 2, 1, 3),
+        hist.transpose(0, 1, 3, 2, 4), upd.transpose(0, 1, 3, 2, 4),
+    )
+    alive = (jnp.arange(blocks) < live[0]).astype(F32)[:, None, None]
+    return (disp + delta).transpose(0, 2, 1, 3), fluid.transpose(1, 0, 2) * alive
 
 
 def solution(mesh):

time: 68.4 us -> 51.6 us (0.75)
  local copies, waits for them, and re-layouts: 13.6 us -> 0 us
  Pallas kernels: 53 us -> 47.1 us
  other arithmetic: 0 us -> 2.93 us
    unnamed x7 -> x0, local copies, waits for them, and re-layouts: 10.8 us -> none
    pallas_call x1, Pallas kernels: 53 us -> 47.1 us  [body(): pl.pallas_call(functools.partial(kernel, nf, ns, (blocks, sub, order, ite...]
    pallas_call x2 -> x0, local copies, waits for them, and re-layouts: 2.84 us -> none  [body(): pl.pallas_call(functools.partial(kernel, nf, ns, (blocks, sub, order, ite...]
    mul x0 -> x1, other arithmetic: none -> 1.61 us  [body(): fluid.transpose(1, 0, 2) * alive]
    transpose x0 -> x1, other arithmetic: none -> 1.32 us  [body(): (disp + delta).transpose(0, 2, 1, 3)]
where the time goes in v2:
time: 51.6 us; the launch traced here: 51.3 us
  Pallas kernels  47.1 us (91%)
  other arithmetic  2.93 us (6%)
  between operations  1.29 us (2%)
    pallas_call x1, Pallas kernels, body(): pl.pallas_call(functools.partial(kernel, nf, ns, (blocks, sub, order, ite...  47.1 us
    mul x1, other arithmetic, body(): fluid.transpose(1, 0, 2) * alive  1.61 us
    transpose x1, other arithmetic, body(): (disp + delta).transpose(0, 2, 1, 3)  1.32 us

profile of v2, /device:TPU:0, one launch (start us, length us, event | category | flops | bytes accessed | tf_op | source)
XLA Modules:
  0.0 51.3 jit_solution(11863434129993393247)
XLA Ops:
  1.3 47.1 %shard_map.113 = (f32[1,3,4,128]{3,2,1,0:T(4,128)}, f32[1,3,4,128]{3,2,1,0:T(4,128)}, f32[3,64,128]{2,1,0:T(8,128)}) custom-call(f32[3,64,128]{2,1,0:T(8,128)} %bitcast.18, f32[3,64,128]{2,1,0:T(8,128)} %bitcast.19, bf16[64,128,128]{2,1,0:T(8,128)(2,1)} %map_hbm.1, s32[1,1]{1,0:T(1,128)} %bitcast.14.live_hbm, s32[1,64]{1,0:T(1,128)} %bitcast.22, ...), custom_call_target="tpu_custom_call" | custom-call | tf_op jit(solution)/shard_map/pallas_call | solution.py:395
  48.4 1.3 %add_bitcast_fusion = f32[1,4,3,128]{3,1,2,0:T(4,128)} fusion(f32[1,3,4,128]{3,2,1,0:T(4,128)} %get-tuple-element.5, f32[1,3,4,128]{3,2,1,0:T(4,128)} %get-tuple-element.6), kind=kLoop, calls=%fused_computation.1 | loop fusion | flops 1536 | bytes 18432 | tf_op jit(solution)/shard_map/transpose | solution.py:449
  49.7 1.6 %multiply_bitcast_fusion = f32[64,3,128]{2,0,1:T(8,128)} fusion(f32[3,64,128]{2,1,0:T(8,128)} %get-tuple-element.7, f32[64]{0:T(128)S(1)} %compare_convert_fusion), kind=kLoop, calls=%fused_computation | loop fusion | flops 24576 | bytes 196864 | tf_op jit(solution)/shard_map/mul | solution.py:449
  (1 shorter events, 0.0 us)
